TPU v7x, 32 devices: a whole 2x2x4 slice. The times are simulated.
32 devices in a mesh: blk: 16 (over z, y, x), phe: 2 (over core).
Axes of the slice: x: 2, y: 2, z: 4, core: 2. Of those that a mesh axis runs over, the one named last changes fastest.
Arguments:
- ld_rows: bfloat16 [16384, 1024], P('blk'), may hold values from -1.5 to 1.5, as said below
- block_first: int32 [16384], P('blk'), may hold values from 0 to 16383, as said below
- beta_hat: float32 [128, 16384], P('phe', 'blk'), may hold values from -6 to 6
- psi: float32 [128, 16384], P('phe', 'blk'), may hold values from 0.05 to 5
- noise: bfloat16 [3, 128, 16384], P(None, 'phe', 'blk'), may hold values from -5 to 5
- sample_size: int32 [128], P('phe'), may hold values from 2000 to 199999
Outputs:
- effects: float32 [128, 16384], P('phe', 'blk')
Inputs may be any that keep to these rules, and one draw needn't show every extreme that they name: block_first[j] is the first SNP of the run of consecutive SNPs that forms j's LD block; every block holds 128 to 1024 SNPs, except the last block, which ends at SNP 16384 - 1 and may hold fewer. ld_rows[j, c] is the LD between SNP j and SNP block_first[j] + c for c below the length of j's block, and zero for larger c; every block's matrix is symmetric with unit diagonal.
All inputs are finite; a program needn't handle non-finite values.
Results may differ from a plain program's by a relative error of at most 0.00055.
The roundings to bfloat16 on the way count: a program that leaves them out, or rounds other values in their place, can miss the bound.
Values may be sent and summed in bfloat16 or wider, within the bound.
No kernel may reach another device: no remote copies, remote signals or barrier semaphores. Data moves between devices by JAX's collectives and lax.ppermute only.
A program may use at most 64 MiB of HBM per device.

v0:
```python
import jax
import jax.numpy as jnp
from jax import lax
from jax.sharding import PartitionSpec as P

ITERS = 3
SLOTS = 10
tiny_term = 1e-06
sample_ref = 20000.0


def extended_2(cells, sides, width):
    for axis, dim in sides:
        count = lax.axis_size(axis)
        ends = count - 1
        head = lax.slice_in_dim(cells, 0, width, axis=dim)
        tail = lax.slice_in_dim(cells, cells.shape[dim] - width, cells.shape[dim], axis=dim)
        cells = jnp.concatenate(
            [
                lax.ppermute(tail, axis, [(i, (i + 1) % count) for i in range(ends)]),
                cells,
                lax.ppermute(head, axis, [((i + 1) % count, i) for i in range(ends)]),
            ],
            axis=dim,
        )
    return cells


def shards(ld_rows, block_first, beta_hat, psi, noise, sample_size):
    snp_local = ld_rows.shape[0]
    span = ld_rows.shape[1]
    pheno_local = beta_hat.shape[0]
    total_snps = snp_local * lax.axis_size("blk")
    total_pheno = pheno_local * lax.axis_size("phe")
    base_row = lax.axis_index("blk") * snp_local
    positions = jnp.arange(snp_local, dtype=jnp.int32)
    start_mask = (block_first == base_row + positions) | (positions == 0)
    seg_first = jnp.nonzero(start_mask, size=SLOTS, fill_value=snp_local)[0].astype(jnp.int32)
    seg_count = jnp.sum(start_mask.astype(jnp.int32))
    seg_next = jnp.concatenate([seg_first[1:], jnp.full((1,), snp_local, jnp.int32)])
    seg_rows = seg_next - seg_first
    clipped = jnp.minimum(seg_first, snp_local - 1)
    seg_col = block_first[clipped] - base_row + span
    ld_padded = jnp.pad(ld_rows, ((0, span), (0, 0)))
    offsets = jnp.arange(span, dtype=jnp.int32)
    beta = jnp.zeros(beta_hat.shape, jnp.float32)
    for iteration in range(ITERS):
        rounded = beta.astype(jnp.bfloat16)
        weighted = beta * beta / psi
        scale_local = jnp.sum(weighted, axis=1)
        scale_total = lax.psum(scale_local, "blk")
        extended = extended_2(rounded, (("blk", 1),), span)

        def one_piece(number, result):
            row_start = seg_first[number]
            ld_tile = lax.dynamic_slice_in_dim(ld_padded, row_start, span, 0)
            window = lax.dynamic_slice_in_dim(extended, seg_col[number], span, 1)
            product = lax.dot_general(
                window, ld_tile, (((1,), (1,)), ((), ())), preferred_element_type=jnp.float32
            )
            product = jnp.where((offsets < seg_rows[number])[None, :], product, jnp.float32(0.0))
            current = lax.dynamic_slice_in_dim(result, row_start, span, 1)
            return lax.dynamic_update_slice_in_dim(result, current + product, row_start, 1)

        start_value = jnp.zeros((pheno_local, snp_local + span), jnp.float32)
        result = lax.fori_loop(0, seg_count, one_piece, start_value)
        applied = result[:, :snp_local]
        grad = beta_hat - applied
        resid_local = jnp.sum(grad * grad, axis=1)
        resid_total = lax.psum(resid_local, "blk")
        pooled_total = lax.psum(jnp.sum(scale_total), "phe")
        pooled = pooled_total / (total_snps * total_pheno) + tiny_term
        scale = scale_total / total_snps + tiny_term
        resid = resid_total / total_snps + tiny_term
        phi = (scale + pooled) / 2.0
        amp = jnp.sqrt(resid * sample_ref / sample_size.astype(jnp.float32))
        shrink = psi / (psi + phi[:, None])
        beta = shrink * (beta + grad + amp[:, None] * noise[iteration].astype(jnp.float32))
    return beta


def solution(mesh):
    in_specs = (
        P("blk", None),
        P("blk"),
        P("phe", "blk"),
        P("phe", "blk"),
        P(None, "phe", "blk"),
        P("phe"),
    )
    out_specs = P("phe", "blk")
    return jax.shard_map(shards, mesh=mesh, in_specs=in_specs, out_specs=out_specs, check_vma=False)
```

profile of v0, /device:TPU:0, one launch (start us, length us, event | category | flops | bytes accessed | tf_op | source)
XLA Modules:
  0.0 288.1 jit_solution(13211630202490944520)
XLA Ops:
  0.0 5.0 %collective-permute-start = (bf16[64,1024]{1,0:T(8,128)(2,1)S(1)}, bf16[64,1024]{1,0:T(8,128)(2,1)S(1)}, u32[]{:S(2)}, u32[]{:S(2)}) collective-permute-start(bf16[64,1024]{1,0:T(8,128)(2,1)S(1)} %convert_element_type.41), channel_id=1, source_target_pairs={{0,2},{2,4},{4,6},{6,8},{8,10},{10,12},{12,14},{14,16},{16,18},{18... | collective-permute-start | bytes 393224 | tf_op jit(solution)/shard_map/ppermute | solution.py:20
  7.6 7.6 %scatter_custom_fusion = s32[10]{0:T(128)S(1)} fusion(s32[1024]{0:T(1024)S(1)} %bitcast.48, s32[1024]{0:T(1024)S(1)} %broadcast.175, s32[]{:T(128)} %constant.110.clone.1), kind=kCustom, calls=%fused_computation.84 | custom fusion | flops 1024 | bytes 44 | tf_op jit(solution)/shard_map/scatter-add | solution.py:38
  16.7 1.3 gather_fusion
  18.8 4.0 %pad.4 = bf16[2048,1024]{1,0:T(8,128)(2,1)} pad(bf16[1024,1024]{1,0:T(8,128)(2,1)} %param.12, bf16[]{:T(256)} %constant.117.clone.1), padding=0_1024x0_0 | pad | bytes 6291458 | tf_op jit(solution)/shard_map/jit(_pad)/pad | solution.py:44
  23.1 30.7 %while.33 = (s32[]{:T(128)}, f32[64,2048]{1,0:T(8,128)S(1)}, s32[]{:T(128)}, s32[10]{0:T(128)S(1)}, s32[10]{0:T(128)S(1)}, /*index=5*/s32[10]{0:T(128)S(1)}, bf1...) while((s32[]{:T(128)}, f32[64,2048]{1,0:T(8,128)S(1)}, ...), condition=%wide.region_10.11_spmd.clone, body=%wide.region_9.10_spmd.clone.sunk | while | flops 134349840 | bytes 3280655 | solution.py:66
  30.0 2.4 fusion.67
  39.5 2.4 fusion.67
  41.9 1.3 dynamic_update_slice.15
  50.0 2.4 fusion.67
  53.9 49.3 %all-reduce.3 = (f32[64]{0:T(128)S(1)}, f32[64]{0:T(128)S(1)}) all-reduce(f32[64]{0:T(128)S(1)} %multiply_reduce_fusion.2, f32[64]{0:T(128)S(1)} %divide_reduce_fusion), channel_id=1, replica_groups=mesh['blk'=16,'phe'=2] {'blk'}, use_global_device_ids=true, to_apply=%region_12.13 | all-reduce | flops 128 | bytes 1024 | tf_op jit(solution)/shard_map/psum | solution.py:70
  103.8 3.1 %psum.64 = f32[]{:T(128)} all-reduce(f32[]{:T(128)} %reduce_sum.95), channel_id=1, replica_groups=mesh['blk'=16,'phe'=2] {'phe'}, use_global_device_ids=true, to_apply=%region_3.4 | all-reduce | flops 1 | bytes 8 | tf_op jit(solution)/shard_map/psum | solution.py:71
  107.9 3.9 %collective-permute-start.2 = (bf16[64,1024]{1,0:T(8,128)(2,1)S(1)}, bf16[64,1024]{1,0:T(8,128)(2,1)S(1)}, u32[]{:S(2)}, u32[]{:S(2)}) collective-permute-start(bf16[64,1024]{1,0:T(8,128)(2,1)S(1)} %convert_element_type.45), channel_id=1, source_target_pairs={{0,2},{2,4},{4,6},{6,8},{8,10},{10,12},{12,14},{14,16},{16,18},{18... | collective-permute-start | bytes 393224 | tf_op jit(solution)/shard_map/ppermute | solution.py:20
  111.8 1.3 collective-permute-start.3
  113.1 4.6 %collective-permute-done.2 = bf16[64,1024]{1,0:T(8,128)(2,1)S(1)} collective-permute-done((bf16[64,1024]{1,0:T(8,128)(2,1)S(1)}, bf16[64,1024]{1,0:T(8,128)(2,1)S(1)}, u32[]{:S(2)}, u32[]{:S(2)}) %collective-permute-start.2) | collective-permute-done | bytes 131104 | tf_op jit(solution)/shard_map/ppermute | solution.py:20
  117.7 1.3 collective-permute-done.3
  119.1 30.6 %while.34 = (s32[]{:T(128)}, f32[64,2048]{1,0:T(8,128)S(1)}, s32[]{:T(128)}, s32[10]{0:T(128)S(1)}, s32[10]{0:T(128)S(1)}, /*index=5*/s32[10]{0:T(128)S(1)}, bf1...) while((s32[]{:T(128)}, f32[64,2048]{1,0:T(8,128)S(1)}, ...), condition=%wide.region_18.19_spmd.clone, body=%wide.region_17.18_spmd.clone.sunk | while | flops 134349840 | bytes 3280655 | solution.py:66
  125.9 2.4 fusion.70
  135.4 2.4 fusion.70
  137.8 1.3 dynamic_update_slice.16
  145.9 2.4 fusion.70
  149.8 43.2 %all-reduce.2 = (f32[64]{0:T(128)S(1)}, f32[64]{0:T(128)S(1)}) all-reduce(f32[64]{0:T(128)S(1)} %multiply_reduce_fusion.1, f32[64]{0:T(128)S(1)} %get-tuple-element.265), channel_id=1, replica_groups=mesh['blk'=16,'phe'=2] {'blk'}, use_global_device_ids=true, to_apply=%region_20.21 | all-reduce | flops 128 | bytes 1024 | tf_op jit(solution)/shard_map/psum | solution.py:70
  193.7 3.1 %psum.67 = f32[]{:T(128)} all-reduce(f32[]{:T(128)} %reduce_sum.99), channel_id=1, replica_groups=mesh['blk'=16,'phe'=2] {'phe'}, use_global_device_ids=true, to_apply=%region_16.17 | all-reduce | flops 1 | bytes 8 | tf_op jit(solution)/shard_map/psum | solution.py:71
  197.7 3.9 %collective-permute-start.4 = (bf16[64,1024]{1,0:T(8,128)(2,1)S(1)}, bf16[64,1024]{1,0:T(8,128)(2,1)S(1)}, u32[]{:S(2)}, u32[]{:S(2)}) collective-permute-start(bf16[64,1024]{1,0:T(8,128)(2,1)S(1)} %convert_element_type.48), channel_id=1, source_target_pairs={{0,2},{2,4},{4,6},{6,8},{8,10},{10,12},{12,14},{14,16},{16,18},{18... | collective-permute-start | bytes 393224 | tf_op jit(solution)/shard_map/ppermute | solution.py:20
  202.9 4.6 %collective-permute-done.4 = bf16[64,1024]{1,0:T(8,128)(2,1)S(1)} collective-permute-done((bf16[64,1024]{1,0:T(8,128)(2,1)S(1)}, bf16[64,1024]{1,0:T(8,128)(2,1)S(1)}, u32[]{:S(2)}, u32[]{:S(2)}) %collective-permute-start.4) | collective-permute-done | bytes 131104 | tf_op jit(solution)/shard_map/ppermute | solution.py:20
  207.5 1.3 collective-permute-done.5
  208.9 30.6 %while.35 = (s32[]{:T(128)}, f32[64,2048]{1,0:T(8,128)S(1)}, s32[]{:T(128)}, s32[10]{0:T(128)S(1)}, s32[10]{0:T(128)S(1)}, /*index=5*/s32[10]{0:T(128)S(1)}, bf1...) while((s32[]{:T(128)}, f32[64,2048]{1,0:T(8,128)S(1)}, ...), condition=%wide.region_26.27_spmd.clone, body=%wide.region_25.26_spmd.clone.sunk | while | flops 134349840 | bytes 3280655 | solution.py:66
  215.7 2.4 fusion.73
  225.2 2.4 fusion.73
  227.6 1.3 dynamic_update_slice.17
  235.7 2.4 fusion.73
  239.6 43.2 %all-reduce.1 = (f32[64]{0:T(128)S(1)}, f32[64]{0:T(128)S(1)}) all-reduce(f32[64]{0:T(128)S(1)} %multiply_reduce_fusion, f32[64]{0:T(128)S(1)} %get-tuple-element.263), channel_id=1, replica_groups=mesh['blk'=16,'phe'=2] {'blk'}, use_global_device_ids=true, to_apply=%region_28.29 | all-reduce | flops 128 | bytes 1024 | tf_op jit(solution)/shard_map/psum | solution.py:70
  283.5 3.1 %psum.70 = f32[]{:T(128)} all-reduce(f32[]{:T(128)} %reduce_sum.102), channel_id=1, replica_groups=mesh['blk'=16,'phe'=2] {'phe'}, use_global_device_ids=true, to_apply=%region_24.25 | all-reduce | flops 1 | bytes 8 | tf_op jit(solution)/shard_map/psum | solution.py:71
  (94 shorter events, 35.9 us)
Async XLA Ops:
  0.0 22.9 %copy-start.1 = (f32[64,1024]{1,0:T(8,128)S(1)}, f32[64,1024]{1,0:T(8,128)}, u32[]{:S(2)}) copy-start(f32[64,1024]{1,0:T(8,128)} %param.15) | copy-start | bytes 786436
  0.0 23.0 %collective-permute-start = (bf16[64,1024]{1,0:T(8,128)(2,1)S(1)}, bf16[64,1024]{1,0:T(8,128)(2,1)S(1)}, u32[]{:S(2)}, u32[]{:S(2)}) collective-permute-start(bf16[64,1024]{1,0:T(8,128)(2,1)S(1)} %convert_element_type.41), channel_id=1, source_target_pairs={{0,2},{2,4},{4,6},{6,8},{8,10},{10,12},{12,14},{14,16},{16,18},{18... | collective-permute-start | bytes 393224 | tf_op jit(solution)/shard_map/ppermute | solution.py:20
  5.0 18.0 %collective-permute-start.1 = (bf16[64,1024]{1,0:T(8,128)(2,1)S(1)}, bf16[64,1024]{1,0:T(8,128)(2,1)S(1)}, u32[]{:S(2)}, u32[]{:S(2)}) collective-permute-start(bf16[64,1024]{1,0:T(8,128)(2,1)S(1)} %convert_element_type.41), channel_id=1, source_target_pairs={{2,0},{4,2},{6,4},{8,6},{10,8},{12,10},{14,12},{16,14},{18,16},{20... | collective-permute-start | bytes 393224 | tf_op jit(solution)/shard_map/ppermute | solution.py:22
  23.1 30.7 %copy-start = (f32[64,1024]{1,0:T(8,128)S(1)}, f32[64,1024]{1,0:T(8,128)}, u32[]{:S(2)}) copy-start(f32[64,1024]{1,0:T(8,128)} %param.14) | copy-start | bytes 786436
  23.1 84.4 %copy-start.3 = (s32[64]{0:T(128)S(1)}, s32[64]{0:T(128)}, u32[]{:S(2)}) copy-start(s32[64]{0:T(128)} %param.17) | copy-start | bytes 772
  23.1 84.5 %copy-start.2 = (bf16[3,64,1024]{2,1,0:T(8,128)(2,1)S(1)}, bf16[3,64,1024]{2,1,0:T(8,128)(2,1)}, u32[]{:S(2)}) copy-start(bf16[3,64,1024]{2,1,0:T(8,128)(2,1)} %param.16) | copy-start | bytes 1179652
  107.9 9.8 %collective-permute-start.2 = (bf16[64,1024]{1,0:T(8,128)(2,1)S(1)}, bf16[64,1024]{1,0:T(8,128)(2,1)S(1)}, u32[]{:S(2)}, u32[]{:S(2)}) collective-permute-start(bf16[64,1024]{1,0:T(8,128)(2,1)S(1)} %convert_element_type.45), channel_id=1, source_target_pairs={{0,2},{2,4},{4,6},{6,8},{8,10},{10,12},{12,14},{14,16},{16,18},{18... | collective-permute-start | bytes 393224 | tf_op jit(solution)/shard_map/ppermute | solution.py:20
  111.8 7.2 %collective-permute-start.3 = (bf16[64,1024]{1,0:T(8,128)(2,1)S(1)}, bf16[64,1024]{1,0:T(8,128)(2,1)S(1)}, u32[]{:S(2)}, u32[]{:S(2)}) collective-permute-start(bf16[64,1024]{1,0:T(8,128)(2,1)S(1)} %convert_element_type.45), channel_id=1, source_target_pairs={{2,0},{4,2},{6,4},{8,6},{10,8},{12,10},{14,12},{16,14},{18,16},{20... | collective-permute-start | bytes 393224 | tf_op jit(solution)/shard_map/ppermute | solution.py:22
  197.7 9.8 %collective-permute-start.4 = (bf16[64,1024]{1,0:T(8,128)(2,1)S(1)}, bf16[64,1024]{1,0:T(8,128)(2,1)S(1)}, u32[]{:S(2)}, u32[]{:S(2)}) collective-permute-start(bf16[64,1024]{1,0:T(8,128)(2,1)S(1)} %convert_element_type.48), channel_id=1, source_target_pairs={{0,2},{2,4},{4,6},{6,8},{8,10},{10,12},{12,14},{14,16},{16,18},{18... | collective-permute-start | bytes 393224 | tf_op jit(solution)/shard_map/ppermute | solution.py:20
  201.6 7.2 %collective-permute-start.5 = (bf16[64,1024]{1,0:T(8,128)(2,1)S(1)}, bf16[64,1024]{1,0:T(8,128)(2,1)S(1)}, u32[]{:S(2)}, u32[]{:S(2)}) collective-permute-start(bf16[64,1024]{1,0:T(8,128)(2,1)S(1)} %convert_element_type.48), channel_id=1, source_target_pairs={{2,0},{4,2},{6,4},{8,6},{10,8},{12,10},{14,12},{16,14},{18,16},{20... | collective-permute-start | bytes 393224 | tf_op jit(solution)/shard_map/ppermute | solution.py:22
where the time goes:
time: 290 us; the launch traced here: 288 us
  blocking collectives  145 us (50%)
  loops' own time  40.7 us (14%)
  local copies, waits for them, and re-layouts  30 us (10%)
  matrix products  21.4 us (7%)
  other arithmetic  20.3 us (7%)
  starting transfers between devices  16.7 us (6%)
  waiting for transfers between devices  11.8 us (4%)
    psum x3, blocking collectives, shards(): resid_total = lax.psum(resid_local, 'blk')  136 us
    another operation x3, loops' own time, shards(): result = lax.fori_loop(0, seg_count, one_piece, start_value)  40.7 us
    dot_general x9, matrix products, one_piece(): lax.dot_general(window, ld_tile, (((1,), (1,)), ((), ())), preferred_elem...  21.4 us
    ppermute x3, starting transfers between devices, extended_2(): lax.ppermute(tail, axis, [(i, (i + 1) % count) for i in range(ends)])  12.9 us
    psum x3, blocking collectives, shards(): pooled_total = lax.psum(jnp.sum(scale_total), 'phe')  9.24 us
    ppermute x3, waiting for transfers between devices, extended_2(): lax.ppermute(tail, axis, [(i, (i + 1) % count) for i in range(ends)])  9.14 us
    scatter-add x1, other arithmetic, shards(): jnp.nonzero(start_mask, size=SLOTS, fill_value=snp_local)[0]  7.61 us
    dynamic_update_slice x9, local copies, waits for them, and re-layouts, one_piece(): lax.dynamic_update_slice_in_dim(result, current + product, row_start, 1)  7.52 us
  transfers between devices with their start and end apart: 6, of which 4 were waited for; matrix products, arithmetic and copies ran while one was open for 6% of the time, Pallas kernels for 0%

commit v1 on v0

--- a/solution.py
+++ b/solution.py
@@ -67,7 +67,13 @@
         applied = result[:, :snp_local]
         grad = beta_hat - applied
         resid_local = jnp.sum(grad * grad, axis=1)
-        resid_total = lax.psum(resid_local, "blk")
+        size = lax.axis_size("blk")
+        resid_total, far = (resid_local, 1)
+        while far < size:
+            resid_total = resid_total + lax.ppermute(
+                resid_total, "blk", [(i_2, i_2 ^ far) for i_2 in range(size)]
+            )
+            far = 2 * far
         pooled_total = lax.psum(jnp.sum(scale_total), "phe")
         pooled = pooled_total / (total_snps * total_pheno) + tiny_term
         scale = scale_total / total_snps + tiny_term

time: 290 us -> 330 us (1.14)
  starting transfers between devices: 16.7 us -> 48 us
  waiting for transfers between devices: 11.8 us -> 38.1 us
  blocking collectives: 145 us -> 127 us
    ppermute x0 -> x12, starting transfers between devices: none -> 35.6 us  [shards(): lax.ppermute(resid_total, 'blk', [(i_2, i_2 ^ far) for i_2 in range(size)])]
    ppermute x0 -> x12, waiting for transfers between devices: none -> 26.9 us  [shards(): lax.ppermute(resid_total, 'blk', [(i_2, i_2 ^ far) for i_2 in range(size)])]
    psum x3, blocking collectives: 136 us -> 118 us  [shards(): scale_total = lax.psum(scale_local, 'blk')]
    ppermute x3, waiting for transfers between devices: 9.14 us -> 4.62 us  [extended_2(): lax.ppermute(tail, axis, [(i, (i + 1) % count) for i in range(ends)])]
    ppermute x3, starting transfers between devices: 12.9 us -> 8.5 us  [extended_2(): lax.ppermute(tail, axis, [(i, (i + 1) % count) for i in range(ends)])]
    ppermute x3, waiting for transfers between devices: 2.62 us -> 6.51 us  [extended_2(): lax.ppermute(head, axis, [((i + 1) % count, i) for i in range(ends)])]
  transfers between devices with their start and end apart: 6 -> 18, of which waited for: 4 -> 12; matrix products, arithmetic and copies ran while one was open for 6% -> 6% of each run, Pallas kernels for 0% -> 0%
where the time goes in v1:
time: 330 us; the launch traced here: 328 us
  blocking collectives  127 us (38%)
  starting transfers between devices  48 us (15%)
  loops' own time  40.7 us (12%)
  waiting for transfers between devices  38.1 us (12%)
  local copies, waits for them, and re-layouts  30 us (9%)
  matrix products  21.4 us (6%)
  other arithmetic  20.3 us (6%)
    psum x3, blocking collectives, shards(): scale_total = lax.psum(scale_local, 'blk')  118 us
    another operation x3, loops' own time, shards(): result = lax.fori_loop(0, seg_count, one_piece, start_value)  40.7 us
    ppermute x12, starting transfers between devices, shards(): lax.ppermute(resid_total, 'blk', [(i_2, i_2 ^ far) for i_2 in range(size)])  35.6 us
    ppermute x12, waiting for transfers between devices, shards(): lax.ppermute(resid_total, 'blk', [(i_2, i_2 ^ far) for i_2 in range(size)])  26.9 us
    dot_general x9, matrix products, one_piece(): lax.dot_general(window, ld_tile, (((1,), (1,)), ((), ())), preferred_elem...  21.4 us
    psum x3, blocking collectives, shards(): pooled_total = lax.psum(jnp.sum(scale_total), 'phe')  9.26 us
    ppermute x3, starting transfers between devices, extended_2(): lax.ppermute(tail, axis, [(i, (i + 1) % count) for i in range(ends)])  8.5 us
    scatter-add x1, other arithmetic, shards(): jnp.nonzero(start_mask, size=SLOTS, fill_value=snp_local)[0]  7.61 us
  transfers between devices with their start and end apart: 18, of which 12 were waited for; matrix products, arithmetic and copies ran while one was open for 6% of the time, Pallas kernels for 0%

profile of v1, /device:TPU:0, one launch (start us, length us, event | category | flops | bytes accessed | tf_op | source)
XLA Modules:
  0.0 327.9 jit_solution(2444971667530388648)
XLA Ops:
  0.0 4.9 %collective-permute-start = (bf16[64,1024]{1,0:T(8,128)(2,1)S(1)}, bf16[64,1024]{1,0:T(8,128)(2,1)S(1)}, u32[]{:S(2)}, u32[]{:S(2)}) collective-permute-start(bf16[64,1024]{1,0:T(8,128)(2,1)S(1)} %convert_element_type.41), channel_id=1, source_target_pairs={{0,2},{2,4},{4,6},{6,8},{8,10},{10,12},{12,14},{14,16},{16,18},{18... | collective-permute-start | bytes 393224 | tf_op jit(solution)/shard_map/ppermute | solution.py:20
  7.5 7.6 %scatter_custom_fusion = s32[10]{0:T(128)S(1)} fusion(s32[1024]{0:T(1024)S(1)} %bitcast.48, s32[1024]{0:T(1024)S(1)} %broadcast.175, s32[]{:T(128)} %constant.110.clone.1), kind=kCustom, calls=%fused_computation.84 | custom fusion | flops 1024 | bytes 44 | tf_op jit(solution)/shard_map/scatter-add | solution.py:38
  18.6 4.0 %pad.4 = bf16[2048,1024]{1,0:T(8,128)(2,1)} pad(bf16[1024,1024]{1,0:T(8,128)(2,1)} %param.12, bf16[]{:T(256)} %constant.117.clone.1), padding=0_1024x0_0 | pad | bytes 6291458 | tf_op jit(solution)/shard_map/jit(_pad)/pad | solution.py:44
  22.9 30.7 %while.33 = (s32[]{:T(128)}, f32[64,2048]{1,0:T(8,128)S(1)}, s32[]{:T(128)}, s32[10]{0:T(128)S(1)}, s32[10]{0:T(128)S(1)}, /*index=5*/s32[10]{0:T(128)S(1)}, bf1...) while((s32[]{:T(128)}, f32[64,2048]{1,0:T(8,128)S(1)}, ...), condition=%wide.region_10.11_spmd.clone, body=%wide.region_9.10_spmd.clone.sunk | while | flops 134349840 | bytes 3280655 | solution.py:66
  29.7 2.4 fusion.67
  39.2 2.4 fusion.67
  49.7 2.4 fusion.67
  53.9 3.4 %collective-permute-done.2 = f32[64]{0:T(128)S(1)} collective-permute-done((f32[64]{0:T(128)S(1)}, f32[64]{0:T(128)S(1)}, u32[]{:S(2)}, u32[]{:S(2)}) %collective-permute-start.2) | collective-permute-done | bytes 288 | tf_op jit(solution)/shard_map/ppermute | solution.py:73
  57.3 13.3 %collective-permute-start.3 = (f32[64]{0:T(128)S(1)}, f32[64]{0:T(128)S(1)}, u32[]{:S(2)}, u32[]{:S(2)}) collective-permute-start(f32[64]{0:T(128)S(1)} %add.256), channel_id=1, source_target_pairs={{0,4},{2,6},{4,0},{6,2},{8,12},{10,14},{12,8},{14,10},{16,20},{18,... | collective-permute-start | bytes 776 | tf_op jit(solution)/shard_map/ppermute | solution.py:73
  70.6 39.6 %psum.42 = f32[64]{0:T(128)S(1)} all-reduce(f32[64]{0:T(128)S(1)} %divide_reduce_fusion), channel_id=1, replica_groups=mesh['blk'=16,'phe'=2] {'blk'}, use_global_device_ids=true, to_apply=%region_1.2 | all-reduce | flops 64 | bytes 512 | tf_op jit(solution)/shard_map/psum | solution.py:51
  110.8 3.1 psum.43
  114.6 4.4 %collective-permute-done.5 = f32[64]{0:T(128)S(1)} collective-permute-done((f32[64]{0:T(128)S(1)}, f32[64]{0:T(128)S(1)}, u32[]{:S(2)}, u32[]{:S(2)}) %collective-permute-start.5) | collective-permute-done | bytes 288 | tf_op jit(solution)/shard_map/ppermute | solution.py:73
  123.2 4.4 %collective-permute-done.7 = bf16[64,1024]{1,0:T(8,128)(2,1)S(1)} collective-permute-done((bf16[64,1024]{1,0:T(8,128)(2,1)S(1)}, bf16[64,1024]{1,0:T(8,128)(2,1)S(1)}, u32[]{:S(2)}, u32[]{:S(2)}) %collective-permute-start.7) | collective-permute-done | bytes 131104 | tf_op jit(solution)/shard_map/ppermute | solution.py:22
  127.7 30.6 %while.34 = (s32[]{:T(128)}, f32[64,2048]{1,0:T(8,128)S(1)}, s32[]{:T(128)}, s32[10]{0:T(128)S(1)}, s32[10]{0:T(128)S(1)}, /*index=5*/s32[10]{0:T(128)S(1)}, bf1...) while((s32[]{:T(128)}, f32[64,2048]{1,0:T(8,128)S(1)}, ...), condition=%wide.region_17.18_spmd.clone, body=%wide.region_16.17_spmd.clone.sunk | while | flops 134349840 | bytes 3280655 | solution.py:66
  134.4 2.4 fusion.70
  144.0 2.4 fusion.70
  154.4 2.4 fusion.70
  158.5 3.6 %collective-permute-done.8 = f32[64]{0:T(128)S(1)} collective-permute-done((f32[64]{0:T(128)S(1)}, f32[64]{0:T(128)S(1)}, u32[]{:S(2)}, u32[]{:S(2)}) %collective-permute-start.8) | collective-permute-done | bytes 288 | tf_op jit(solution)/shard_map/ppermute | solution.py:73
  162.0 13.2 %collective-permute-start.9 = (f32[64]{0:T(128)S(1)}, f32[64]{0:T(128)S(1)}, u32[]{:S(2)}, u32[]{:S(2)}) collective-permute-start(f32[64]{0:T(128)S(1)} %add.269), channel_id=1, source_target_pairs={{0,4},{2,6},{4,0},{6,2},{8,12},{10,14},{12,8},{14,10},{16,20},{18,... | collective-permute-start | bytes 776 | tf_op jit(solution)/shard_map/ppermute | solution.py:73
  176.8 38.2 %psum.44 = f32[64]{0:T(128)S(1)} all-reduce(f32[64]{0:T(128)S(1)} %get-tuple-element.259), channel_id=1, replica_groups=mesh['blk'=16,'phe'=2] {'blk'}, use_global_device_ids=true, to_apply=%region_13.14 | all-reduce | flops 64 | bytes 512 | tf_op jit(solution)/shard_map/psum | solution.py:51
  215.6 3.1 psum.45
  219.4 4.4 %collective-permute-done.11 = f32[64]{0:T(128)S(1)} collective-permute-done((f32[64]{0:T(128)S(1)}, f32[64]{0:T(128)S(1)}, u32[]{:S(2)}, u32[]{:S(2)}) %collective-permute-start.11) | collective-permute-done | bytes 288 | tf_op jit(solution)/shard_map/ppermute | solution.py:73
  227.8 3.4 %collective-permute-done.12 = bf16[64,1024]{1,0:T(8,128)(2,1)S(1)} collective-permute-done((bf16[64,1024]{1,0:T(8,128)(2,1)S(1)}, bf16[64,1024]{1,0:T(8,128)(2,1)S(1)}, u32[]{:S(2)}, u32[]{:S(2)}) %collective-permute-start.12) | collective-permute-done | bytes 131104 | tf_op jit(solution)/shard_map/ppermute | solution.py:20
  233.4 30.6 %while.35 = (s32[]{:T(128)}, f32[64,2048]{1,0:T(8,128)S(1)}, s32[]{:T(128)}, s32[10]{0:T(128)S(1)}, s32[10]{0:T(128)S(1)}, /*index=5*/s32[10]{0:T(128)S(1)}, bf1...) while((s32[]{:T(128)}, f32[64,2048]{1,0:T(8,128)S(1)}, ...), condition=%wide.region_24.25_spmd.clone, body=%wide.region_23.24_spmd.clone.sunk | while | flops 134349840 | bytes 3280655 | solution.py:66
  240.2 2.4 fusion.73
  249.7 2.4 fusion.73
  260.2 2.4 fusion.73
  264.2 3.6 %collective-permute-done.14 = f32[64]{0:T(128)S(1)} collective-permute-done((f32[64]{0:T(128)S(1)}, f32[64]{0:T(128)S(1)}, u32[]{:S(2)}, u32[]{:S(2)}) %collective-permute-start.14) | collective-permute-done | bytes 288 | tf_op jit(solution)/shard_map/ppermute | solution.py:73
  267.8 8.7 %collective-permute-start.15 = (f32[64]{0:T(128)S(1)}, f32[64]{0:T(128)S(1)}, u32[]{:S(2)}, u32[]{:S(2)}) collective-permute-start(f32[64]{0:T(128)S(1)} %add.282), channel_id=1, source_target_pairs={{0,4},{2,6},{4,0},{6,2},{8,12},{10,14},{12,8},{14,10},{16,20},{18,... | collective-permute-start | bytes 776 | tf_op jit(solution)/shard_map/ppermute | solution.py:73
  278.1 40.1 %psum.46 = f32[64]{0:T(128)S(1)} all-reduce(f32[64]{0:T(128)S(1)} %get-tuple-element.257), channel_id=1, replica_groups=mesh['blk'=16,'phe'=2] {'blk'}, use_global_device_ids=true, to_apply=%region_20.21 | all-reduce | flops 64 | bytes 512 | tf_op jit(solution)/shard_map/psum | solution.py:51
  318.8 3.1 psum.47
  322.6 4.4 %collective-permute-done.17 = f32[64]{0:T(128)S(1)} collective-permute-done((f32[64]{0:T(128)S(1)}, f32[64]{0:T(128)S(1)}, u32[]{:S(2)}, u32[]{:S(2)}) %collective-permute-start.17) | collective-permute-done | bytes 288 | tf_op jit(solution)/shard_map/ppermute | solution.py:73
  (127 shorter events, 53.0 us)
Async XLA Ops:
  0.0 22.7 %collective-permute-start = (bf16[64,1024]{1,0:T(8,128)(2,1)S(1)}, bf16[64,1024]{1,0:T(8,128)(2,1)S(1)}, u32[]{:S(2)}, u32[]{:S(2)}) collective-permute-start(bf16[64,1024]{1,0:T(8,128)(2,1)S(1)} %convert_element_type.41), channel_id=1, source_target_pairs={{0,2},{2,4},{4,6},{6,8},{8,10},{10,12},{12,14},{14,16},{16,18},{18... | collective-permute-start | bytes 393224 | tf_op jit(solution)/shard_map/ppermute | solution.py:20
  4.9 17.8 %collective-permute-start.1 = (bf16[64,1024]{1,0:T(8,128)(2,1)S(1)}, bf16[64,1024]{1,0:T(8,128)(2,1)S(1)}, u32[]{:S(2)}, u32[]{:S(2)}) collective-permute-start(bf16[64,1024]{1,0:T(8,128)(2,1)S(1)} %convert_element_type.41), channel_id=1, source_target_pairs={{2,0},{4,2},{6,4},{8,6},{10,8},{12,10},{14,12},{16,14},{18,16},{20... | collective-permute-start | bytes 393224 | tf_op jit(solution)/shard_map/ppermute | solution.py:22
  22.8 30.7 %copy-start = (f32[64,1024]{1,0:T(8,128)S(1)}, f32[64,1024]{1,0:T(8,128)}, u32[]{:S(2)}) copy-start(f32[64,1024]{1,0:T(8,128)} %param.14) | copy-start | bytes 786436
  22.8 30.9 %copy-start.1 = (f32[64,1024]{1,0:T(8,128)S(1)}, f32[64,1024]{1,0:T(8,128)}, u32[]{:S(2)}) copy-start(f32[64,1024]{1,0:T(8,128)} %param.15) | copy-start | bytes 786436
  22.8 96.3 %copy-start.3 = (s32[64]{0:T(128)S(1)}, s32[64]{0:T(128)}, u32[]{:S(2)}) copy-start(s32[64]{0:T(128)} %param.17) | copy-start | bytes 772
  22.8 96.3 %copy-start.2 = (bf16[3,64,1024]{2,1,0:T(8,128)(2,1)S(1)}, bf16[3,64,1024]{2,1,0:T(8,128)(2,1)}, u32[]{:S(2)}) copy-start(bf16[3,64,1024]{2,1,0:T(8,128)(2,1)} %param.16) | copy-start | bytes 1179652
  53.7 3.6 %collective-permute-start.2 = (f32[64]{0:T(128)S(1)}, f32[64]{0:T(128)S(1)}, u32[]{:S(2)}, u32[]{:S(2)}) collective-permute-start(f32[64]{0:T(128)S(1)} %multiply_reduce_fusion.2), channel_id=1, source_target_pairs={{0,2},{2,0},{4,6},{6,4},{8,10},{10,8},{12,14},{14,12},{16,18},{18,... | collective-permute-start | bytes 776 | tf_op jit(solution)/shard_map/ppermute | solution.py:73
  57.3 53.5 %collective-permute-start.3 = (f32[64]{0:T(128)S(1)}, f32[64]{0:T(128)S(1)}, u32[]{:S(2)}, u32[]{:S(2)}) collective-permute-start(f32[64]{0:T(128)S(1)} %add.256), channel_id=1, source_target_pairs={{0,4},{2,6},{4,0},{6,2},{8,12},{10,14},{12,8},{14,10},{16,20},{18,... | collective-permute-start | bytes 776 | tf_op jit(solution)/shard_map/ppermute | solution.py:73
  110.8 3.8 %collective-permute-start.4 = (f32[64]{0:T(128)S(1)}, f32[64]{0:T(128)S(1)}, u32[]{:S(2)}, u32[]{:S(2)}) collective-permute-start(f32[64]{0:T(128)S(1)} %add.257), channel_id=1, source_target_pairs={{0,8},{2,10},{4,12},{6,14},{8,0},{10,2},{12,4},{14,6},{16,24},{18,... | collective-permute-start | bytes 776 | tf_op jit(solution)/shard_map/ppermute | solution.py:73
  114.6 4.5 %collective-permute-start.5 = (f32[64]{0:T(128)S(1)}, f32[64]{0:T(128)S(1)}, u32[]{:S(2)}, u32[]{:S(2)}) collective-permute-start(f32[64]{0:T(128)S(1)} %add.258), channel_id=1, source_target_pairs={{0,16},{2,18},{4,20},{6,22},{8,24},{10,26},{12,28},{14,30},{16,0},... | collective-permute-start | bytes 776 | tf_op jit(solution)/shard_map/ppermute | solution.py:73
  119.4 3.8 %collective-permute-start.6 = (bf16[64,1024]{1,0:T(8,128)(2,1)S(1)}, bf16[64,1024]{1,0:T(8,128)(2,1)S(1)}, u32[]{:S(2)}, u32[]{:S(2)}) collective-permute-start(bf16[64,1024]{1,0:T(8,128)(2,1)S(1)} %convert_element_type.45), channel_id=1, source_target_pairs={{0,2},{2,4},{4,6},{6,8},{8,10},{10,12},{12,14},{14,16},{16,18},{18... | collective-permute-start | bytes 393224 | tf_op jit(solution)/shard_map/ppermute | solution.py:20
  120.7 6.9 %collective-permute-start.7 = (bf16[64,1024]{1,0:T(8,128)(2,1)S(1)}, bf16[64,1024]{1,0:T(8,128)(2,1)S(1)}, u32[]{:S(2)}, u32[]{:S(2)}) collective-permute-start(bf16[64,1024]{1,0:T(8,128)(2,1)S(1)} %convert_element_type.45), channel_id=1, source_target_pairs={{2,0},{4,2},{6,4},{8,6},{10,8},{12,10},{14,12},{16,14},{18,16},{20... | collective-permute-start | bytes 393224 | tf_op jit(solution)/shard_map/ppermute | solution.py:22
  158.4 3.6 %collective-permute-start.8 = (f32[64]{0:T(128)S(1)}, f32[64]{0:T(128)S(1)}, u32[]{:S(2)}, u32[]{:S(2)}) collective-permute-start(f32[64]{0:T(128)S(1)} %multiply_reduce_fusion.1), channel_id=1, source_target_pairs={{0,2},{2,0},{4,6},{6,4},{8,10},{10,8},{12,14},{14,12},{16,18},{18,... | collective-permute-start | bytes 776 | tf_op jit(solution)/shard_map/ppermute | solution.py:73
  162.0 14.8 %collective-permute-start.9 = (f32[64]{0:T(128)S(1)}, f32[64]{0:T(128)S(1)}, u32[]{:S(2)}, u32[]{:S(2)}) collective-permute-start(f32[64]{0:T(128)S(1)} %add.269), channel_id=1, source_target_pairs={{0,4},{2,6},{4,0},{6,2},{8,12},{10,14},{12,8},{14,10},{16,20},{18,... | collective-permute-start | bytes 776 | tf_op jit(solution)/shard_map/ppermute | solution.py:73
  176.8 42.5 %collective-permute-start.10 = (f32[64]{0:T(128)S(1)}, f32[64]{0:T(128)S(1)}, u32[]{:S(2)}, u32[]{:S(2)}) collective-permute-start(f32[64]{0:T(128)S(1)} %add.270), channel_id=1, source_target_pairs={{0,8},{2,10},{4,12},{6,14},{8,0},{10,2},{12,4},{14,6},{16,24},{18,... | collective-permute-start | bytes 776 | tf_op jit(solution)/shard_map/ppermute | solution.py:73
  219.3 4.5 %collective-permute-start.11 = (f32[64]{0:T(128)S(1)}, f32[64]{0:T(128)S(1)}, u32[]{:S(2)}, u32[]{:S(2)}) collective-permute-start(f32[64]{0:T(128)S(1)} %add.271), channel_id=1, source_target_pairs={{0,16},{2,18},{4,20},{6,22},{8,24},{10,26},{12,28},{14,30},{16,0},... | collective-permute-start | bytes 776 | tf_op jit(solution)/shard_map/ppermute | solution.py:73
  224.2 7.1 %collective-permute-start.12 = (bf16[64,1024]{1,0:T(8,128)(2,1)S(1)}, bf16[64,1024]{1,0:T(8,128)(2,1)S(1)}, u32[]{:S(2)}, u32[]{:S(2)}) collective-permute-start(bf16[64,1024]{1,0:T(8,128)(2,1)S(1)} %convert_element_type.48), channel_id=1, source_target_pairs={{0,2},{2,4},{4,6},{6,8},{8,10},{10,12},{12,14},{14,16},{16,18},{18... | collective-permute-start | bytes 393224 | tf_op jit(solution)/shard_map/ppermute | solution.py:20
  226.5 6.9 %collective-permute-start.13 = (bf16[64,1024]{1,0:T(8,128)(2,1)S(1)}, bf16[64,1024]{1,0:T(8,128)(2,1)S(1)}, u32[]{:S(2)}, u32[]{:S(2)}) collective-permute-start(bf16[64,1024]{1,0:T(8,128)(2,1)S(1)} %convert_element_type.48), channel_id=1, source_target_pairs={{2,0},{4,2},{6,4},{8,6},{10,8},{12,10},{14,12},{16,14},{18,16},{20... | collective-permute-start | bytes 393224 | tf_op jit(solution)/shard_map/ppermute | solution.py:22
  264.2 3.6 %collective-permute-start.14 = (f32[64]{0:T(128)S(1)}, f32[64]{0:T(128)S(1)}, u32[]{:S(2)}, u32[]{:S(2)}) collective-permute-start(f32[64]{0:T(128)S(1)} %multiply_reduce_fusion), channel_id=1, source_target_pairs={{0,2},{2,0},{4,6},{6,4},{8,10},{10,8},{12,14},{14,12},{16,18},{18,... | collective-permute-start | bytes 776 | tf_op jit(solution)/shard_map/ppermute | solution.py:73
  267.8 10.3 %collective-permute-start.15 = (f32[64]{0:T(128)S(1)}, f32[64]{0:T(128)S(1)}, u32[]{:S(2)}, u32[]{:S(2)}) collective-permute-start(f32[64]{0:T(128)S(1)} %add.282), channel_id=1, source_target_pairs={{0,4},{2,6},{4,0},{6,2},{8,12},{10,14},{12,8},{14,10},{16,20},{18,... | collective-permute-start | bytes 776 | tf_op jit(solution)/shard_map/ppermute | solution.py:73
  278.1 44.5 %collective-permute-start.16 = (f32[64]{0:T(128)S(1)}, f32[64]{0:T(128)S(1)}, u32[]{:S(2)}, u32[]{:S(2)}) collective-permute-start(f32[64]{0:T(128)S(1)} %add.283), channel_id=1, source_target_pairs={{0,8},{2,10},{4,12},{6,14},{8,0},{10,2},{12,4},{14,6},{16,24},{18,... | collective-permute-start | bytes 776 | tf_op jit(solution)/shard_map/ppermute | solution.py:73
  322.5 4.5 %collective-permute-start.17 = (f32[64]{0:T(128)S(1)}, f32[64]{0:T(128)S(1)}, u32[]{:S(2)}, u32[]{:S(2)}) collective-permute-start(f32[64]{0:T(128)S(1)} %add.284), channel_id=1, source_target_pairs={{0,16},{2,18},{4,20},{6,22},{8,24},{10,26},{12,28},{14,30},{16,0},... | collective-permute-start | bytes 776 | tf_op jit(solution)/shard_map/ppermute | solution.py:73
